TPU v7x, 32 devices: a whole 2x2x4 slice. The times are simulated.
32 devices in a mesh: dp: 2 (over x), ctx: 4 (over y, core), tp: 4 (over z).
Axes of the slice: x: 2, y: 2, z: 4, core: 2. Of those that a mesh axis runs over, the one named last changes fastest.
Arguments:
- block_input: bfloat16 [2, 8, 256, 2048], P('dp', 'ctx', 'tp'), may hold values from -6 to 6
- block_order: int32 [2, 8], P('dp'), may hold values from 0 to 7, each once within a row
- w_qkv: bfloat16 [2048, 3, 2048], P(('dp', 'ctx'), None, 'tp'), may hold values from -1 to 1
- w_out: bfloat16 [2048, 2048], P('tp', ('dp', 'ctx')), may hold values from -3 to 3
- gain_attn: bfloat16 [2048], P(('dp', 'ctx')), may hold values from 0.5 to 1.5
- w_gate_up: bfloat16 [2048, 2, 8192], P(('dp', 'ctx'), None, 'tp'), may hold values from -0.125 to 0.125
- w_down: bfloat16 [8192, 2048], P('tp', ('dp', 'ctx')), may hold values from -0.0625 to 0.0625
- gain_mlp: bfloat16 [2048], P(('dp', 'ctx')), may hold values from 0.5 to 1.5
- cotangent: bfloat16 [2, 8, 256, 2048], P('dp', 'ctx', 'tp'), may hold values from -6 to 6
Outputs:
- block_output: bfloat16 [2, 8, 256, 2048], P('dp', 'ctx', 'tp')
- input_grad: float32 [2, 8, 256, 2048], P('dp', 'ctx', 'tp')
- grad_qkv: float32 [2048, 3, 2048], P(('dp', 'ctx'), None, 'tp')
- grad_out: float32 [2048, 2048], P('tp', ('dp', 'ctx'))
- grad_gain_attn: float32 [2048], P(('dp', 'ctx'))
- grad_gate_up: float32 [2048, 2, 8192], P(('dp', 'ctx'), None, 'tp')
- grad_down: float32 [8192, 2048], P('tp', ('dp', 'ctx'))
- grad_gain_mlp: float32 [2048], P(('dp', 'ctx'))
Inputs may be any that keep to these rules, and one draw needn't show every extreme that they name: `block_order`: each row lists every block number of one sequence once.
All inputs are finite; a program needn't handle non-finite values.
Results may differ from a plain program's by a relative error of at most 0.019.
Values may be sent and summed in bfloat16 or wider, within the bound.
A program may use at most 192 MiB of HBM per device.

v0:
```python
import jax
import jax.numpy as jnp
from jax import lax
from jax.sharding import PartitionSpec as P

HEAD_DIM = 64
EPSILON = 1e-05
ROPE_BASE = 130000.0
NEG_LARGE = -1e30


def rope_tables(positions, head_size):
    half = head_size // 2
    freq = ROPE_BASE ** (-(jnp.arange(half, dtype=jnp.float32) * 2.0 / head_size))
    angle = positions.astype(jnp.float32)[..., None] * freq
    cosine = jnp.cos(angle)
    sine = jnp.sin(angle)
    return (jnp.concatenate([cosine, cosine], -1), jnp.concatenate([sine, sine], -1))


def rotate(values):
    half = values.shape[-1] // 2
    return jnp.concatenate([-values[..., half:], values[..., :half]], -1)


def unrotate(values):
    half = values.shape[-1] // 2
    return jnp.concatenate([values[..., half:], -values[..., :half]], -1)


def rope_apply(values, cosine, sine):
    return values * cosine + rotate(values) * sine


def rope_back(grads, cosine, sine):
    return grads * cosine + unrotate(grads * sine)


def gather_rows(values):
    return lax.all_gather(values, "tp", axis=2, tiled=True)


def sum_rows(values):
    return lax.psum_scatter(values, "tp", scatter_dimension=2, tiled=True)


def gather_cotangent(values):
    return lax.all_gather(values, "tp", axis=2, tiled=True)


def sum_normed(values):
    return lax.psum_scatter(values, "tp", scatter_dimension=2, tiled=True)


def block_scores(query, key_blk, query_pos, key_pos, head_count):
    key_heads = key_blk.reshape(key_blk.shape[0], head_count, HEAD_DIM)
    scores = jnp.einsum("qhe,khe->hqk", query, key_heads, preferred_element_type=jnp.float32)
    visible = key_pos[None, :] <= query_pos[:, None]
    return jnp.where(visible[None], scores, -jnp.inf)


def online_update(state, query, query_pos, key_blk, value_blk, key_pos, head_count):
    run_max, run_sum, run_acc = state
    scores = block_scores(query, key_blk, query_pos, key_pos, head_count)
    new_max = jnp.maximum(run_max, jnp.max(scores, -1))
    factor = jnp.exp(run_max - new_max)
    probs = jnp.exp(scores - new_max[..., None])
    new_sum = run_sum * factor + jnp.sum(probs, -1)
    value_heads = value_blk.reshape(value_blk.shape[0], head_count, HEAD_DIM).astype(jnp.float32)
    mixed = jnp.einsum("hqk,khe->qhe", probs, value_heads, precision=lax.Precision.HIGHEST)
    new_acc = run_acc * factor.T[:, :, None] + mixed
    return (new_max, new_sum, new_acc)


def backward_block(
    query, query_pos, grad_blk, log_total, delta, key_blk, value_blk, key_pos, head_count
):
    scores = block_scores(query, key_blk, query_pos, key_pos, head_count)
    probs = jnp.exp(scores - log_total[..., None])
    value_heads = value_blk.reshape(value_blk.shape[0], head_count, HEAD_DIM)
    key_heads = key_blk.reshape(key_blk.shape[0], head_count, HEAD_DIM)
    dprobs = jnp.einsum("qhe,khe->hqk", grad_blk, value_heads, preferred_element_type=jnp.float32)
    grad_scores = (probs * (dprobs - delta[..., None])).astype(jnp.bfloat16)
    grad_query = jnp.einsum(
        "hqk,khe->qhe", grad_scores, key_heads, preferred_element_type=jnp.float32
    )
    grad_key = jnp.einsum("hqk,qhe->khe", grad_scores, query, preferred_element_type=jnp.float32)
    grad_value = jnp.einsum(
        "hqk,qhe->khe", probs.astype(jnp.bfloat16), grad_blk, preferred_element_type=jnp.float32
    )
    flat_width = head_count * HEAD_DIM
    return (grad_query, grad_key.reshape(-1, flat_width), grad_value.reshape(-1, flat_width))


def body(block_input, block_order, w_qkv, w_out, gain_attn, w_gate_up, w_down, gain_mlp, cotangent):
    f32 = jnp.float32
    bf16 = jnp.bfloat16
    seq_count = block_input.shape[0]
    row_count = block_input.shape[2]
    span = row_count * lax.axis_size("tp")
    local_width = w_qkv.shape[2]
    head_count = local_width // HEAD_DIM
    query_rows = 2 * span
    block_total = block_order.shape[1]
    ctx_index = lax.axis_index("ctx")
    my_ids = lax.dynamic_slice_in_dim(block_order, ctx_index * 2, 2, 1)
    offsets = jnp.arange(span, dtype=jnp.int32)
    query_pos = (my_ids[:, :, None] * span + offsets).reshape(seq_count, query_rows)
    cosine, sine = rope_tables(query_pos, HEAD_DIM)
    cosine = cosine[:, :, None, :]
    sine = sine[:, :, None, :]
    full_qkv, full_out, full_gain_attn = (
        lax.all_gather(w_qkv, ("dp", "ctx"), axis=0, tiled=True),
        lax.all_gather(w_out, ("dp", "ctx"), axis=1, tiled=True),
        lax.all_gather(gain_attn, ("dp", "ctx"), axis=0, tiled=True),
    )
    x_float = block_input.astype(f32)
    rms_attn = lax.rsqrt(jnp.mean(x_float * x_float, -1, keepdims=True) + EPSILON)
    unit_attn = x_float * rms_attn
    normed_attn = (unit_attn * full_gain_attn.astype(f32)).astype(bf16)
    normed_attn_full = gather_rows(normed_attn)
    qkv = jnp.einsum("spcd,dte->spcte", normed_attn_full, full_qkv, preferred_element_type=f32)
    qkv = qkv.reshape(seq_count, query_rows, 3, head_count, HEAD_DIM)
    queries = (rope_apply(qkv[:, :, 0], cosine, sine) * 0.125).astype(bf16)
    keys = rope_apply(qkv[:, :, 1], cosine, sine).astype(bf16)
    values = qkv[:, :, 2].astype(bf16)
    key_send = keys.reshape(seq_count, 2, span, local_width)
    value_send = values.reshape(seq_count, 2, span, local_width)
    initial = (
        jnp.full((seq_count, head_count, query_rows), NEG_LARGE, f32),
        jnp.zeros((seq_count, head_count, query_rows), f32),
        jnp.zeros((seq_count, query_rows, head_count, HEAD_DIM), f32),
    )
    key_piece = lax.all_gather(key_send, "ctx", axis=1, tiled=True)
    value_piece = lax.all_gather(value_send, "ctx", axis=1, tiled=True)

    def visit(step_index, inner):
        run_max, run_sum, run_acc = inner
        key_ids = lax.dynamic_index_in_dim(block_order, step_index, 1, False)
        key_blk = lax.dynamic_index_in_dim(key_piece, step_index, 1, False)
        value_blk = lax.dynamic_index_in_dim(value_piece, step_index, 1, False)
        member = 0
        key_pos = key_ids[member] * span + offsets
        operands = (run_max[member], run_sum[member], run_acc[member])

        def update(current, member=member, key_pos=key_pos):
            return online_update(
                current,
                queries[member],
                query_pos[member],
                key_blk[member],
                value_blk[member],
                key_pos,
                head_count,
            )

        result = update(operands)
        maxes = [result[0]]
        sums = [result[1]]
        accs = [result[2]]
        return (jnp.stack(maxes), jnp.stack(sums), jnp.stack(accs))

    run_max, run_sum, run_acc = lax.fori_loop(0, key_piece.shape[1], visit, initial)
    attention = (run_acc / jnp.transpose(run_sum, (0, 2, 1))[..., None]).astype(bf16)
    log_total = run_max + jnp.log(run_sum)
    attn_flat = attention.reshape(seq_count, 2, span, local_width)
    attn_part = jnp.einsum("spce,ed->spcd", attn_flat, full_out, preferred_element_type=f32)
    resid_mid = x_float + sum_rows(attn_part)
    full_gate_up, full_down, full_gain_mlp = (
        lax.all_gather(w_gate_up, ("dp", "ctx"), axis=0, tiled=True),
        lax.all_gather(w_down, ("dp", "ctx"), axis=1, tiled=True),
        lax.all_gather(gain_mlp, ("dp", "ctx"), axis=0, tiled=True),
    )
    rms_mlp = lax.rsqrt(jnp.mean(resid_mid * resid_mid, -1, keepdims=True) + EPSILON)
    unit_mlp = resid_mid * rms_mlp
    normed_mlp = (unit_mlp * full_gain_mlp.astype(f32)).astype(bf16)
    normed_mlp_full = gather_rows(normed_mlp)
    gate_up = jnp.einsum(
        "spcd,dtf->spctf", normed_mlp_full, full_gate_up, preferred_element_type=f32
    )
    gate = gate_up[:, :, :, 0]
    upper = gate_up[:, :, :, 1]
    sigma = jax.nn.sigmoid(gate)
    hidden = (gate * sigma * upper).astype(bf16)
    down_part = jnp.einsum("spcf,fd->spcd", hidden, full_down, preferred_element_type=f32)
    resid_out = resid_mid + sum_rows(down_part)
    block_output = resid_out.astype(bf16)
    back_gate_up, back_down, back_gain_mlp = (full_gate_up, full_down, full_gain_mlp)
    back_qkv, back_out, back_gain_attn = (full_qkv, full_out, full_gain_attn)
    cotan_full = gather_cotangent(cotangent)
    grad_down_local = jnp.einsum("spcf,spcd->fd", hidden, cotan_full, preferred_element_type=f32)
    grad_hidden = jnp.einsum("spcd,fd->spcf", cotan_full, back_down, preferred_element_type=f32)
    act_grad = jnp.stack(
        [grad_hidden * upper * sigma * (1.0 + gate * (1.0 - sigma)), grad_hidden * gate * sigma],
        axis=3,
    ).astype(bf16)
    grad_gate_up_local = jnp.einsum(
        "spcd,spctf->dtf", normed_mlp_full, act_grad, preferred_element_type=f32
    )
    grad_normed_mlp = sum_normed(
        jnp.einsum("spctf,dtf->spcd", act_grad, back_gate_up, preferred_element_type=f32)
    )
    gain_term_mlp = jnp.sum(grad_normed_mlp * unit_mlp, axis=(0, 1, 2))
    scaled_two = grad_normed_mlp * back_gain_mlp.astype(f32)
    grad_mid = cotangent.astype(f32) + rms_mlp * (
        scaled_two - unit_mlp * jnp.mean(scaled_two * unit_mlp, -1, keepdims=True)
    )
    mlp_shares = (
        lax.psum_scatter(
            grad_gate_up_local.astype(jnp.bfloat16), ("dp", "ctx"), scatter_dimension=0, tiled=True
        ).astype(jnp.float32),
        lax.psum_scatter(
            grad_down_local.astype(jnp.bfloat16), ("dp", "ctx"), scatter_dimension=1, tiled=True
        ).astype(jnp.float32),
        lax.psum_scatter(
            gain_term_mlp.astype(jnp.bfloat16), ("dp", "ctx"), scatter_dimension=0, tiled=True
        ).astype(jnp.float32),
    )
    grad_mid_b = grad_mid.astype(bf16)
    mid_full = gather_cotangent(grad_mid_b)
    grad_out_local = jnp.einsum("spce,spcd->ed", attn_flat, mid_full, preferred_element_type=f32)
    grad_attention = jnp.einsum(
        "spcd,ed->spce", mid_full, back_out, preferred_element_type=f32
    ).astype(bf16)
    grad_attention = grad_attention.reshape(seq_count, query_rows, head_count, HEAD_DIM)
    delta = jnp.transpose(
        jnp.sum(grad_attention.astype(f32) * attention.astype(f32), -1), (0, 2, 1)
    )
    all_keys, all_values = (
        lax.all_gather(key_send, "ctx", axis=1, tiled=True),
        lax.all_gather(value_send, "ctx", axis=1, tiled=True),
    )

    def back_step(grad_queries, slot):
        key_ids = lax.dynamic_index_in_dim(block_order, slot, 1, False)
        key_blk = lax.dynamic_index_in_dim(all_keys, slot, 1, False)
        value_blk = lax.dynamic_index_in_dim(all_values, slot, 1, False)
        member = 0
        key_pos = key_ids[member] * span + offsets

        def work(current, member=member, key_pos=key_pos):
            grad_query, grad_key, grad_value = backward_block(
                queries[member],
                query_pos[member],
                grad_attention[member],
                log_total[member],
                delta[member],
                key_blk[member],
                value_blk[member],
                key_pos,
                head_count,
            )
            return (current + grad_query, grad_key, grad_value)

        result = work(grad_queries[member])
        query_list = [result[0]]
        key_list = [result[1]]
        value_list = [result[2]]
        return (jnp.stack(query_list), (jnp.stack(key_list), jnp.stack(value_list)))

    start_grads = jnp.zeros((seq_count, query_rows, head_count, HEAD_DIM), f32)
    grad_queries, (key_terms, value_terms) = lax.scan(
        back_step, start_grads, jnp.arange(block_total, dtype=jnp.int32)
    )
    grad_keys, grad_values = (
        lax.psum_scatter(
            key_terms.astype(jnp.bfloat16), "ctx", scatter_dimension=0, tiled=True
        ).astype(jnp.float32),
        lax.psum_scatter(
            value_terms.astype(jnp.bfloat16), "ctx", scatter_dimension=0, tiled=True
        ).astype(jnp.float32),
    )
    grad_keys = jnp.transpose(grad_keys, (1, 0, 2, 3)).reshape(
        seq_count, query_rows, head_count, HEAD_DIM
    )
    grad_values = jnp.transpose(grad_values, (1, 0, 2, 3)).reshape(
        seq_count, query_rows, head_count, HEAD_DIM
    )
    qkv_grad = jnp.stack(
        [
            rope_back(grad_queries, cosine, sine) * 0.125,
            rope_back(grad_keys, cosine, sine),
            grad_values,
        ],
        axis=2,
    ).astype(bf16)
    qkv_grad = qkv_grad.reshape(seq_count, 2, span, 3, local_width)
    grad_qkv_local = jnp.einsum(
        "spcd,spcte->dte", normed_attn_full, qkv_grad, preferred_element_type=f32
    )
    grad_normed_attn = sum_normed(
        jnp.einsum("spcte,dte->spcd", qkv_grad, back_qkv, preferred_element_type=f32)
    )
    gain_term_attn = jnp.sum(grad_normed_attn * unit_attn, axis=(0, 1, 2))
    scaled_one = grad_normed_attn * back_gain_attn.astype(f32)
    input_grad = grad_mid + rms_attn * (
        scaled_one - unit_attn * jnp.mean(scaled_one * unit_attn, -1, keepdims=True)
    )
    shard_qkv, shard_out, shard_gain_attn = (
        lax.psum_scatter(
            grad_qkv_local.astype(jnp.bfloat16), ("dp", "ctx"), scatter_dimension=0, tiled=True
        ).astype(jnp.float32),
        lax.psum_scatter(
            grad_out_local.astype(jnp.bfloat16), ("dp", "ctx"), scatter_dimension=1, tiled=True
        ).astype(jnp.float32),
        lax.psum_scatter(
            gain_term_attn.astype(jnp.bfloat16), ("dp", "ctx"), scatter_dimension=0, tiled=True
        ).astype(jnp.float32),
    )
    shard_gate_up, shard_down, shard_gain_mlp = mlp_shares
    total_gain_attn, total_gain_mlp = lax.psum((shard_gain_attn, shard_gain_mlp), "tp")
    return (
        block_output,
        input_grad,
        shard_qkv,
        shard_out,
        total_gain_attn,
        shard_gate_up,
        shard_down,
        total_gain_mlp,
    )


def solution(mesh):
    in_specs = (
        P("dp", "ctx", "tp", None),
        P("dp", None),
        P(("dp", "ctx"), None, "tp"),
        P("tp", ("dp", "ctx")),
        P(("dp", "ctx")),
        P(("dp", "ctx"), None, "tp"),
        P("tp", ("dp", "ctx")),
        P(("dp", "ctx")),
        P("dp", "ctx", "tp", None),
    )
    out_specs = (
        P("dp", "ctx", "tp", None),
        P("dp", "ctx", "tp", None),
        P(("dp", "ctx"), None, "tp"),
        P("tp", ("dp", "ctx")),
        P(("dp", "ctx")),
        P(("dp", "ctx"), None, "tp"),
        P("tp", ("dp", "ctx")),
        P(("dp", "ctx")),
    )
    return jax.shard_map(body, mesh=mesh, in_specs=in_specs, out_specs=out_specs, check_vma=False)
```

profile of v0, /device:TPU:0, one launch (start us, length us, event | category | flops | bytes accessed | tf_op | source)
XLA Modules:
  0.0 1424.0 jit_solution(8658560242486038990)
XLA Ops:
  27.8 30.2 %all-gather.15.cloned.1.call-done = bf16[2048,3,512]{2,0,1:T(8,128)(2,1)} async-done(((bf16[256,3,512]{2,0,1:T(8,128)(2,1)}), bf16[2048,3,512]{2,0,1:T(8,128)(2,1)}) %all-gather.15.cloned.1.call-update) | async-done | bytes 6291472 | tf_op jit(solution)/shard_map/all_gather | solution.py:113
  66.9 39.0 %all-gather.13.cloned.1.call-done = bf16[1,2,256,2048]{3,2,1,0:T(8,128)(2,1)} async-done(((bf16[1,2,64,2048]{3,2,1,0:T(8,128)(2,1)}), bf16[1,2,256,2048]{3,2,1,0:T(8,128)(2,1)}) %all-gather.13.cloned.1.call-update) | async-done | bytes 2097168 | tf_op jit(solution)/shard_map/all_gather | solution.py:40
  133.6 15.4 %all-gather.17.cloned.1.call-done = bf16[1,8,256,512]{3,2,0,1:T(8,128)(2,1)} async-done(((bf16[1,2,256,512]{3,2,0,1:T(8,128)(2,1)}), bf16[1,8,256,512]{3,2,0,1:T(8,128)(2,1)}) %all-gather.17.cloned.1.call-update) | async-done | bytes 2097168 | tf_op jit(solution)/shard_map/all_gather | solution.py:134
  152.9 20.7 %all-gather.19.cloned.1.call-done = bf16[1,8,256,512]{3,2,0,1:T(8,128)(2,1)} async-done(((bf16[1,2,256,512]{3,2,0,1:T(8,128)(2,1)}), bf16[1,8,256,512]{3,2,0,1:T(8,128)(2,1)}) %all-gather.19.cloned.1.call-update) | async-done | bytes 2097168 | tf_op jit(solution)/shard_map/all_gather | solution.py:135
  177.6 92.5 %while.34 = (s32[]{:T(128)}, f32[1,8,512]{2,1,0:T(8,128)S(1)}, f32[1,8,512]{2,1,0:T(8,128)S(1)}, f32[1,512,8,64]{1,3,2,0:T(8,128)S(1)}, s32[1,8]{1,0:T(1,128)S(1...) while((s32[]{:T(128)}, f32[1,8,512]{2,1,0:T(8,128)S(1)}, ...), condition=%wide.region_4.5_spmd.clone, body=%wide.region_1.4_spmd.clone.sunk | while | flops 947548928 | bytes 34334904 | solution.py:163
  285.1 67.6 %reduce-scatter.11.cloned.1.call-done = f32[1,2,64,2048]{3,2,1,0:T(8,128)} async-done(((f32[1,2,256,2048]{3,2,1,0:T(8,128)}), f32[1,2,64,2048]{3,2,1,0:T(8,128)}) %reduce-scatter.11.cloned.1.call-update) | async-done | bytes 1048592 | tf_op jit(solution)/shard_map/reduce_scatter | solution.py:44
  361.0 40.7 %all-gather.23.cloned.1.call-done = bf16[1,2,256,2048]{3,2,1,0:T(8,128)(2,1)} async-done(((bf16[1,2,64,2048]{3,2,1,0:T(8,128)(2,1)}), bf16[1,2,256,2048]{3,2,1,0:T(8,128)(2,1)}) %all-gather.23.cloned.1.call-update) | async-done | bytes 2097168 | tf_op jit(solution)/shard_map/all_gather | solution.py:40
  401.7 91.0 %all-gather.25.cloned.1.call-done = bf16[2048,2,2048]{2,0,1:T(8,128)(2,1)} async-done(((bf16[256,2,2048]{2,0,1:T(8,128)(2,1)}), bf16[2048,2,2048]{2,0,1:T(8,128)(2,1)}) %all-gather.25.cloned.1.call-update) | async-done | bytes 16777232 | tf_op jit(solution)/shard_map/all_gather | solution.py:170
  492.7 15.1 %fusion.48 = f32[1,2,256,2,2048]{4,2,3,1,0:T(8,128)} fusion(bf16[2048,2,2048]{2,0,1:T(8,128)(2,1)} %all-gather.25.cloned.1.call-done, bf16[1,2,256,2048]{3,2,1,0:T(8,128)(2,1)} %all-gather.23.cloned.1.call-done), kind=kOutput, calls=%fused_computation.71 | convolution fusion | flops 8589934592 | bytes 27262976 | tf_op jit(solution)/shard_map/spcd,dtf->spctf/dot_general | solution.py:178
  507.8 32.2 %all-gather.29.cloned.1.call-done = bf16[1,2,256,2048]{3,2,1,0:T(8,128)(2,1)} async-done(((bf16[1,2,64,2048]{3,2,1,0:T(8,128)(2,1)}), bf16[1,2,256,2048]{3,2,1,0:T(8,128)(2,1)}) %all-gather.29.cloned.1.call-update) | async-done | bytes 2097168 | tf_op jit(solution)/shard_map/all_gather | solution.py:48
  540.0 56.4 %all-gather.27.cloned.1.call-done = bf16[2048,2048]{1,0:T(8,128)(2,1)} async-done(((bf16[2048,256]{1,0:T(8,128)(2,1)}), bf16[2048,2048]{1,0:T(8,128)(2,1)}) %all-gather.27.cloned.1.call-update) | async-done | bytes 8388624 | tf_op jit(solution)/shard_map/all_gather | solution.py:171
  609.8 13.8 fusion.54
  623.6 76.9 %reduce-scatter.15.cloned.1.call-done = f32[1,2,64,2048]{3,2,1,0:T(8,128)} async-done(((f32[1,2,256,2048]{3,2,1,0:T(8,128)}), f32[1,2,64,2048]{3,2,1,0:T(8,128)}) %reduce-scatter.15.cloned.1.call-update) | async-done | bytes 1048592 | tf_op jit(solution)/shard_map/reduce_scatter | solution.py:52
  704.7 46.0 %all-gather.31.cloned.1.call-done = bf16[1,2,256,2048]{3,2,1,0:T(8,128)(2,1)} async-done(((bf16[1,2,64,2048]{3,2,1,0:T(8,128)(2,1)}), bf16[1,2,256,2048]{3,2,1,0:T(8,128)(2,1)}) %all-gather.31.cloned.1.call-update) | async-done | bytes 2097168 | tf_op jit(solution)/shard_map/all_gather | solution.py:48
  760.7 122.6 %while.35 = (s32[]{:T(128)}, f32[1,512,8,64]{1,3,2,0:T(8,128)}, bf16[8,1,256,512]{3,2,0,1:T(8,128)(2,1)}, bf16[8,1,256,512]{3,2,0,1:T(8,128)(2,1)}, s32[8]{0:T(1...) while((s32[]{:T(128)}, f32[1,512,8,64]{1,3,2,0:T(8,128)}, ...), condition=%wide.wide.region_12.13_spmd.clone, body=%wide.wide.region_11.12_spmd.clone.sunk | while | flops 679871232 | bytes 27977976 | solution.py:262
  927.3 20.3 %reduce-scatter.19.cloned.1.call-done = bf16[2,1,256,512]{3,2,0,1:T(8,128)(2,1)} async-done(((bf16[8,1,256,512]{3,2,0,1:T(8,128)(2,1)}), bf16[2,1,256,512]{3,2,0,1:T(8,128)(2,1)}) %reduce-scatter.19.cloned.1.call-update) | async-done | bytes 524304 | tf_op jit(solution)/shard_map/reduce_scatter | solution.py:269
  978.7 14.6 %bitcast_convert_fusion = bf16[2048,2,2048]{2,0,1:T(8,128)(2,1)} fusion(bf16[2,256,1,2048]{3,1,0,2:T(8,128)(2,1)} %copy-done.35, bf16[2,256,1,2048]{3,1,0,2:T(8,128)(2,1)} %copy-done.34, bf16[1,2,256,2048]{3,2,1,0:T(8,128)(2,1)S(1)} %copy-done.28), kind=kOutput, calls=%fused_computation.58 | convolution fusion | flops 8606711808 | bytes 23068672 | tf_op jit(solution)/shard_map/spcd,spctf->dtf/dot_general | solution.py:197
  995.2 27.0 %reduce-scatter.29.cloned.1.call-done = bf16[2048,256]{1,0:T(8,128)(2,1)} async-done(((bf16[2048,2048]{1,0:T(8,128)(2,1)}), bf16[2048,256]{1,0:T(8,128)(2,1)}) %reduce-scatter.29.cloned.1.call-update) | async-done | bytes 1048592 | tf_op jit(solution)/shard_map/reduce_scatter | solution.py:212
  1024.9 41.6 %reduce-scatter.25.cloned.1.call-done = bf16[512,256]{1,0:T(8,128)(2,1)} async-done(((bf16[512,2048]{1,0:T(8,128)(2,1)}), bf16[512,256]{1,0:T(8,128)(2,1)}) %reduce-scatter.25.cloned.1.call-update) | async-done | bytes 262160 | tf_op jit(solution)/shard_map/reduce_scatter | solution.py:303
  1068.3 77.8 %reduce-scatter.21.cloned.1.call-done = f32[1,2,64,2048]{3,2,1,0:T(8,128)} async-done(((f32[1,2,256,2048]{3,2,1,0:T(8,128)}), f32[1,2,64,2048]{3,2,1,0:T(8,128)}) %reduce-scatter.21.cloned.1.call-update) | async-done | bytes 1048592 | tf_op jit(solution)/shard_map/reduce_scatter | solution.py:52
  1147.7 13.6 all-reduce.3
  1173.9 51.9 %reduce-scatter.13.cloned.1.call-done = f32[1,2,64,2048]{3,2,1,0:T(8,128)} async-done(((f32[1,2,256,2048]{3,2,1,0:T(8,128)}), f32[1,2,64,2048]{3,2,1,0:T(8,128)}) %reduce-scatter.13.cloned.1.call-update) | async-done | bytes 1048592 | tf_op jit(solution)/shard_map/reduce_scatter | solution.py:44
  1228.9 62.4 %reduce-scatter.23.cloned.1.call-done = bf16[256,3,512]{2,0,1:T(8,128)(2,1)} async-done(((bf16[2048,3,512]{2,0,1:T(8,128)(2,1)}), bf16[256,3,512]{2,0,1:T(8,128)(2,1)}) %reduce-scatter.23.cloned.1.call-update) | async-done | bytes 786448 | tf_op jit(solution)/shard_map/reduce_scatter | solution.py:300
  1293.8 117.1 %reduce-scatter.27.cloned.1.call-done = bf16[256,2,2048]{2,0,1:T(8,128)(2,1)} async-done(((bf16[2048,2,2048]{2,0,1:T(8,128)(2,1)}), bf16[256,2,2048]{2,0,1:T(8,128)(2,1)}) %reduce-scatter.27.cloned.1.call-update) | async-done | bytes 2097168 | tf_op jit(solution)/shard_map/reduce_scatter | solution.py:209
  (435 shorter events, 422.9 us)
Async XLA Ops:
  7.2 50.9 %all-gather.15.cloned.1.call-start = ((), (), s32[]{:S(2)}) async-start(), calls=%async_computation.11 | async-start | bytes 7077888 | tf_op jit(solution)/shard_map/all_gather | solution.py:113
  7.9 98.0 %all-gather.13.cloned.1.call-start = ((), (), s32[]{:S(2)}) async-start(), calls=%async_computation.10 | async-start | bytes 2621440 | tf_op jit(solution)/shard_map/all_gather | solution.py:40
  23.0 126.0 %all-gather.17.cloned.1.call-start = ((), (), s32[]{:S(2)}) async-start(), calls=%async_computation.12 | async-start | bytes 2621440 | tf_op jit(solution)/shard_map/all_gather | solution.py:134
  127.5 46.1 %all-gather.19.cloned.1.call-start = ((), (), s32[]{:S(2)}) async-start(), calls=%async_computation.13 | async-start | bytes 2621440 | tf_op jit(solution)/shard_map/all_gather | solution.py:135
  131.1 139.3 %all-gather.21.cloned.1.call-start = ((), (), s32[]{:S(2)}) async-start(), calls=%async_computation.14 | async-start | bytes 2359296 | tf_op jit(solution)/shard_map/all_gather | solution.py:114
  131.7 221.0 %reduce-scatter.11.cloned.1.call-start = ((), (), s32[]{:S(2)}) async-start(), calls=%async_computation.15 | async-start | bytes 5242880 | tf_op jit(solution)/shard_map/reduce_scatter | solution.py:44
  275.5 126.2 %all-gather.23.cloned.1.call-start = ((), (), s32[]{:S(2)}) async-start(), calls=%async_computation.16 | async-start | bytes 2621440 | tf_op jit(solution)/shard_map/all_gather | solution.py:40
  354.2 347.9 %copy-start.1 = (f32[1,2,64,2048]{3,2,1,0:T(8,128)}, f32[1,2,64,2048]{3,2,1,0:T(8,128)S(1)}, u32[]{:S(2)}) copy-start(f32[1,2,64,2048]{3,2,1,0:T(8,128)S(1)} %get-tuple-element.460) | copy-start | bytes 3145732
  355.4 137.4 %all-gather.25.cloned.1.call-start = ((), (), s32[]{:S(2)}) async-start(), calls=%async_computation.17 | async-start | bytes 18874368 | tf_op jit(solution)/shard_map/all_gather | solution.py:170
  359.2 180.8 %all-gather.29.cloned.1.call-start = ((), (), s32[]{:S(2)}) async-start(), calls=%async_computation.20 | async-start | bytes 2621440 | tf_op jit(solution)/shard_map/all_gather | solution.py:48
  360.0 236.4 %all-gather.27.cloned.1.call-start = ((), (), s32[]{:S(2)}) async-start(), calls=%async_computation.18 | async-start | bytes 9437184 | tf_op jit(solution)/shard_map/all_gather | solution.py:171
  360.6 339.9 %reduce-scatter.15.cloned.1.call-start = ((), (), s32[]{:S(2)}) async-start(), calls=%async_computation.21 | async-start | bytes 5242880 | tf_op jit(solution)/shard_map/reduce_scatter | solution.py:52
  623.6 127.2 %all-gather.31.cloned.1.call-start = ((), (), s32[]{:S(2)}) async-start(), calls=%async_computation.22 | async-start | bytes 2621440 | tf_op jit(solution)/shard_map/all_gather | solution.py:48
  704.5 208.9 %reduce-scatter.17.cloned.1.call-start = ((), (), s32[]{:S(2)}) async-start(), calls=%async_computation.23 | async-start | bytes 2621440 | tf_op jit(solution)/shard_map/reduce_scatter | solution.py:266
  883.3 64.3 %reduce-scatter.19.cloned.1.call-start = ((), (), s32[]{:S(2)}) async-start(), calls=%async_computation.24 | async-start | bytes 2621440 | tf_op jit(solution)/shard_map/reduce_scatter | solution.py:269
  883.9 138.4 %reduce-scatter.29.cloned.1.call-start = ((), (), s32[]{:S(2)}) async-start(), calls=%async_computation.29 | async-start | bytes 9437184 | tf_op jit(solution)/shard_map/reduce_scatter | solution.py:212
  893.3 173.2 %reduce-scatter.25.cloned.1.call-start = ((), (), s32[]{:S(2)}) async-start(), calls=%async_computation.27 | async-start | bytes 2359296 | tf_op jit(solution)/shard_map/reduce_scatter | solution.py:303
  898.5 247.6 %reduce-scatter.21.cloned.1.call-start = ((), (), s32[]{:S(2)}) async-start(), calls=%async_computation.25 | async-start | bytes 5242880 | tf_op jit(solution)/shard_map/reduce_scatter | solution.py:52
  956.2 269.6 %reduce-scatter.13.cloned.1.call-start = ((), (), s32[]{:S(2)}) async-start(), calls=%async_computation.19 | async-start | bytes 5242880 | tf_op jit(solution)/shard_map/reduce_scatter | solution.py:44
  969.0 322.3 %reduce-scatter.23.cloned.1.call-start = ((), (), s32[]{:S(2)}) async-start(), calls=%async_computation.26 | async-start | bytes 7077888 | tf_op jit(solution)/shard_map/reduce_scatter | solution.py:300
  977.1 433.8 %reduce-scatter.27.cloned.1.call-start = ((), (), s32[]{:S(2)}) async-start(), calls=%async_computation.28 | async-start | bytes 18874368 | tf_op jit(solution)/shard_map/reduce_scatter | solution.py:209
  993.4 232.4 %copy-start.2 = (f32[1,2,64,2048]{3,2,1,0:T(8,128)S(1)}, f32[1,2,64,2048]{3,2,1,0:T(8,128)}, u32[]{:S(2)}) copy-start(f32[1,2,64,2048]{3,2,1,0:T(8,128)} %copy-done.1) | copy-start | bytes 3145732
  993.4 232.4 %copy-start.7 = (f32[1,2,64,2048]{3,2,1,0:T(8,128)S(1)}, f32[1,2,64,2048]{3,2,1,0:T(8,128)}, u32[]{:S(2)}) copy-start(f32[1,2,64,2048]{3,2,1,0:T(8,128)} %reduce-scatter.15.cloned.1.call-done) | copy-start | bytes 3145732
  993.4 232.4 %copy-start.9 = (bf16[1,2,64,2048]{3,2,1,0:T(8,128)(2,1)S(1)}, bf16[1,2,64,2048]{3,2,1,0:T(8,128)(2,1)}, u32[]{:S(2)}) copy-start(bf16[1,2,64,2048]{3,2,1,0:T(8,128)(2,1)} %param.21) | copy-start | bytes 1572868
  (39 other events, 1022.6 us)
Sparse Core Ops, SparseCore 0:
  9.9 48.1 all-gather.14
  60.2 45.6 all-gather.12
  127.6 21.3 all-gather.16
  151.0 22.5 all-gather.18
  175.3 28.0 all-gather.20
  275.6 77.0 reduce-scatter.10
  355.5 46.1 all-gather.22
  404.2 88.5 all-gather.24
  494.3 45.6 all-gather.28
  541.7 54.6 all-gather.26
  623.7 76.7 reduce-scatter.14
  704.6 46.1 all-gather.30
  883.4 29.9 reduce-scatter.16
  916.4 31.1 reduce-scatter.18
  950.9 71.2 reduce-scatter.28
  1025.3 41.1 reduce-scatter.24
  1069.2 76.7 reduce-scatter.20
  1148.2 77.5 reduce-scatter.12
  1229.2 62.0 reduce-scatter.22
  1294.7 116.1 reduce-scatter.26
where the time goes:
time: 1430 us; the launch traced here: 1420 us
  waiting for transfers between devices  931 us (65%)
  matrix products  222 us (16%)
  local copies, waits for them, and re-layouts  109 us (8%)
  other arithmetic  85.4 us (6%)
  blocking collectives  45.4 us (3%)
  between operations  16 us (1%)
    reduce_scatter x2, waiting for transfers between devices, sum_normed(): return lax.psum_scatter(values, 'tp', scatter_dimension=2, tiled=True)  155 us
    reduce_scatter x2, waiting for transfers between devices, sum_rows(): return lax.psum_scatter(values, 'tp', scatter_dimension=2, tiled=True)  119 us
    reduce_scatter x1, waiting for transfers between devices, body(): lax.psum_scatter(grad_gate_up_local.astype(jnp.bfloat16), ('dp', 'ctx'),...  117 us
    all_gather x1, waiting for transfers between devices, body(): lax.all_gather(w_gate_up, ('dp', 'ctx'), axis=0, tiled=True)  91 us
    all_gather x2, waiting for transfers between devices, gather_rows(): return lax.all_gather(values, 'tp', axis=2, tiled=True)  79.7 us
    all_gather x2, waiting for transfers between devices, gather_cotangent(): return lax.all_gather(values, 'tp', axis=2, tiled=True)  78.2 us
    reduce_scatter x1, waiting for transfers between devices, body(): lax.psum_scatter(grad_qkv_local.astype(jnp.bfloat16), ('dp', 'ctx'), scat...  62.4 us
    all_gather x1, waiting for transfers between devices, body(): lax.all_gather(w_down, ('dp', 'ctx'), axis=1, tiled=True)  56.4 us
  transfers between devices with their start and end apart: 20, of which 19 were waited for; matrix products, arithmetic and copies ran while one was open for 15% of the time, Pallas kernels for 0%

commit v1 on v0

--- a/solution.py
+++ b/solution.py
@@ -7,6 +7,28 @@
 EPSILON = 1e-05
 ROPE_BASE = 130000.0
 NEG_LARGE = -1e30
+
+
+def laid_out(parts, dim):
+    parts = jnp.moveaxis(parts, 0, dim)
+    shape = parts.shape
+    return parts.reshape(*shape[:dim], shape[dim] * shape[dim + 1], *shape[dim + 2 :])
+
+
+def grow_blocks(x, axis):
+    size = lax.axis_size(axis)
+    blocks = x[None]
+    for level in range(size.bit_length() - 1):
+        stride = 1 << level
+        theirs = lax.ppermute(blocks, axis, [(i, i ^ stride) for i in range(size)])
+        both = jnp.stack([blocks, theirs])
+        upper = lax.axis_index(axis) >> level & 1
+        blocks = jnp.where(upper == 0, both, both[::-1]).reshape(-1, *x.shape)
+    return blocks
+
+
+def doubled_up(value, axis, dim):
+    return laid_out(grow_blocks(value, axis), dim)
 
 
 def rope_tables(positions, head_size):
@@ -37,7 +59,7 @@
 
 
 def gather_rows(values):
-    return lax.all_gather(values, "tp", axis=2, tiled=True)
+    return doubled_up(values, "tp", 2)
 
 
 def sum_rows(values):

time: 1430 us -> 1380 us (0.965)
  waiting for transfers between devices: 931 us -> 864 us
    ppermute x0 -> x4, waiting for transfers between devices: none -> 110 us  [grow_blocks(): theirs = lax.ppermute(blocks, axis, [(i, i ^ stride) for i in range(size)])]
    all_gather x2 -> x0, waiting for transfers between devices: 79.7 us -> none  [gather_rows(): return lax.all_gather(values, 'tp', axis=2, tiled=True)]
    all_gather x1, waiting for transfers between devices: 91 us -> 27 us  [body(): lax.all_gather(w_gate_up, ('dp', 'ctx'), axis=0, tiled=True)]
    all_gather x1, waiting for transfers between devices: 30.2 us -> 0.01 us  [body(): lax.all_gather(w_qkv, ('dp', 'ctx'), axis=0, tiled=True)]
    unnamed x80 -> x84, local copies, waits for them, and re-layouts: 29.5 us -> 30 us
  transfers between devices with their start and end apart: 20 -> 22, of which waited for: 19 -> 20; matrix products, arithmetic and copies ran while one was open for 15% -> 16% of each run, Pallas kernels for 0% -> 0%
where the time goes in v1:
time: 1380 us; the launch traced here: 1370 us
  waiting for transfers between devices  864 us (63%)
  matrix products  220 us (16%)
  local copies, waits for them, and re-layouts  113 us (8%)
  other arithmetic  86.5 us (6%)
  blocking collectives  45.8 us (3%)
  loops' own time  16.1 us (1%)
  between operations  16 us (1%)
    reduce_scatter x2, waiting for transfers between devices, sum_normed(): return lax.psum_scatter(values, 'tp', scatter_dimension=2, tiled=True)  154 us
    reduce_scatter x1, waiting for transfers between devices, body(): lax.psum_scatter(grad_gate_up_local.astype(jnp.bfloat16), ('dp', 'ctx'),...  117 us
    reduce_scatter x2, waiting for transfers between devices, sum_rows(): return lax.psum_scatter(values, 'tp', scatter_dimension=2, tiled=True)  114 us
    ppermute x4, waiting for transfers between devices, grow_blocks(): theirs = lax.ppermute(blocks, axis, [(i, i ^ stride) for i in range(size)])  110 us
    all_gather x2, waiting for transfers between devices, gather_cotangent(): return lax.all_gather(values, 'tp', axis=2, tiled=True)  78.4 us
    reduce_scatter x1, waiting for transfers between devices, body(): lax.psum_scatter(grad_qkv_local.astype(jnp.bfloat16), ('dp', 'ctx'), scat...  62.2 us
    all_gather x1, waiting for transfers between devices, body(): lax.all_gather(w_down, ('dp', 'ctx'), axis=1, tiled=True)  56.6 us
    reduce_scatter x1, waiting for transfers between devices, body(): lax.psum_scatter(grad_out_local.astype(jnp.bfloat16), ('dp', 'ctx'), scat...  41.6 us
  transfers between devices with their start and end apart: 22, of which 20 were waited for; matrix products, arithmetic and copies ran while one was open for 16% of the time, Pallas kernels for 0%

profile of v1, /device:TPU:0, one launch (start us, length us, event | category | flops | bytes accessed | tf_op | source)
XLA Modules:
  0.0 1372.1 jit_solution(13812420750441696035)
XLA Ops:
  43.1 41.3 %collective-permute-done.1 = bf16[2,1,2,64,2048]{4,3,2,0,1:T(8,128)(2,1)} collective-permute-done((bf16[2,1,2,64,2048]{4,3,2,0,1:T(8,128)(2,1)S(1)}, bf16[2,1,2,64,2048]{4,3,2,0,1:T(8,128)(2,1)}, u32[]{:S(2)}, u32[]{:S(2)}) %collective-permute-start.1) | collective-permute-done | bytes 1048608 | tf_op jit(solution)/shard_map/ppermute | solution.py:23
  124.5 16.9 %all-gather.13.cloned.1.call-done = bf16[1,8,256,512]{3,2,0,1:T(8,128)(2,1)} async-done(((bf16[1,2,256,512]{3,2,0,1:T(8,128)(2,1)}), bf16[1,8,256,512]{3,2,0,1:T(8,128)(2,1)}) %all-gather.13.cloned.1.call-update) | async-done | bytes 2097168 | tf_op jit(solution)/shard_map/all_gather | solution.py:156
  145.3 20.8 %all-gather.15.cloned.1.call-done = bf16[1,8,256,512]{3,2,0,1:T(8,128)(2,1)} async-done(((bf16[1,2,256,512]{3,2,0,1:T(8,128)(2,1)}), bf16[1,8,256,512]{3,2,0,1:T(8,128)(2,1)}) %all-gather.15.cloned.1.call-update) | async-done | bytes 2097168 | tf_op jit(solution)/shard_map/all_gather | solution.py:157
  170.1 92.6 %while.34 = (s32[]{:T(128)}, f32[1,8,512]{2,1,0:T(8,128)S(1)}, f32[1,8,512]{2,1,0:T(8,128)S(1)}, f32[1,512,8,64]{1,3,2,0:T(8,128)S(1)}, s32[1,8]{1,0:T(1,128)S(1...) while((s32[]{:T(128)}, f32[1,8,512]{2,1,0:T(8,128)S(1)}, ...), condition=%wide.region_4.5_spmd.clone, body=%wide.region_1.4_spmd.clone.sunk | while | flops 947548928 | bytes 34334904 | solution.py:185
  283.0 62.4 %reduce-scatter.11.cloned.1.call-done = f32[1,2,64,2048]{3,2,1,0:T(8,128)} async-done(((f32[1,2,256,2048]{3,2,1,0:T(8,128)}), f32[1,2,64,2048]{3,2,1,0:T(8,128)}) %reduce-scatter.11.cloned.1.call-update) | async-done | bytes 1048592 | tf_op jit(solution)/shard_map/reduce_scatter | solution.py:66
  364.0 44.7 %collective-permute-done.3 = bf16[2,1,2,64,2048]{4,3,2,0,1:T(8,128)(2,1)S(1)} collective-permute-done((bf16[2,1,2,64,2048]{4,3,2,0,1:T(8,128)(2,1)S(1)}, bf16[2,1,2,64,2048]{4,3,2,0,1:T(8,128)(2,1)S(1)}, u32[]{:S(2)}, u32[]{:S(2)}) %collective-permute-start.3) | collective-permute-done | bytes 1048608 | tf_op jit(solution)/shard_map/ppermute | solution.py:23
  411.0 27.0 %all-gather.19.cloned.1.call-done = bf16[2048,2,2048]{2,0,1:T(8,128)(2,1)} async-done(((bf16[256,2,2048]{2,0,1:T(8,128)(2,1)}), bf16[2048,2,2048]{2,0,1:T(8,128)(2,1)}) %all-gather.19.cloned.1.call-update) | async-done | bytes 16777232 | tf_op jit(solution)/shard_map/all_gather | solution.py:192
  438.0 15.1 %fusion.48 = f32[1,2,256,2,2048]{4,2,3,1,0:T(8,128)} fusion(bf16[2,256,2048,1]{2,1,3,0:T(8,128)(2,1)} %bitcast.463, bf16[2048,2,2048]{2,0,1:T(8,128)(2,1)} %all-gather.19.cloned.1.call-done), kind=kOutput, calls=%fused_computation.71 | convolution fusion | flops 8589934592 | bytes 27262976 | tf_op jit(solution)/shard_map/spcd,dtf->spctf/dot_general | solution.py:200
  453.0 32.2 %all-gather.23.cloned.1.call-done = bf16[1,2,256,2048]{3,2,1,0:T(8,128)(2,1)} async-done(((bf16[1,2,64,2048]{3,2,1,0:T(8,128)(2,1)}), bf16[1,2,256,2048]{3,2,1,0:T(8,128)(2,1)}) %all-gather.23.cloned.1.call-update) | async-done | bytes 2097168 | tf_op jit(solution)/shard_map/all_gather | solution.py:70
  485.2 56.6 %all-gather.21.cloned.1.call-done = bf16[2048,2048]{1,0:T(8,128)(2,1)} async-done(((bf16[2048,256]{1,0:T(8,128)(2,1)}), bf16[2048,2048]{1,0:T(8,128)(2,1)}) %all-gather.21.cloned.1.call-update) | async-done | bytes 8388624 | tf_op jit(solution)/shard_map/all_gather | solution.py:193
  555.1 13.8 %fusion.54 = f32[1,2,256,2048]{3,2,1,0:T(8,128)} fusion(bf16[2048,2,2048]{2,0,1:T(8,128)(2,1)} %all-gather.19.cloned.1.call-done, bf16[2,256,1,2048]{3,1,0,2:T(8,128)(2,1)S(1)} %get-tuple-element.470, bf16[2,256,1,2048]{3,1,0,2:T(8,128)(2,1)S(1)} %get-tuple-element.469), kind=kOutput, calls=%fused_computation.81 | convolution fusion | flops 8592031744 | bytes 25165824 | tf_op jit(solution)/shard_map/spctf,dtf->spcd/dot_general | solution.py:223
  569.1 76.7 %reduce-scatter.15.cloned.1.call-done = f32[1,2,64,2048]{3,2,1,0:T(8,128)} async-done(((f32[1,2,256,2048]{3,2,1,0:T(8,128)}), f32[1,2,64,2048]{3,2,1,0:T(8,128)}) %reduce-scatter.15.cloned.1.call-update) | async-done | bytes 1048592 | tf_op jit(solution)/shard_map/reduce_scatter | solution.py:74
  648.8 46.2 %all-gather.25.cloned.1.call-done = bf16[1,2,256,2048]{3,2,1,0:T(8,128)(2,1)} async-done(((bf16[1,2,64,2048]{3,2,1,0:T(8,128)(2,1)}), bf16[1,2,256,2048]{3,2,1,0:T(8,128)(2,1)}) %all-gather.25.cloned.1.call-update) | async-done | bytes 2097168 | tf_op jit(solution)/shard_map/all_gather | solution.py:70
  704.9 126.4 %while.35 = (s32[]{:T(128)}, f32[1,512,8,64]{1,3,2,0:T(8,128)}, bf16[8,1,256,512]{3,2,0,1:T(8,128)(2,1)}, bf16[8,1,256,512]{3,2,0,1:T(8,128)(2,1)}, s32[8]{0:T(1...) while((s32[]{:T(128)}, f32[1,512,8,64]{1,3,2,0:T(8,128)}, ...), condition=%wide.wide.region_12.13_spmd.clone, body=%wide.wide.region_11.12_spmd.clone.sunk | while | flops 679871232 | bytes 27977976 | solution.py:284
  848.4 13.1 reduce-scatter.17.cloned.1.call-done
  875.3 20.3 %reduce-scatter.19.cloned.1.call-done = bf16[2,1,256,512]{3,2,0,1:T(8,128)(2,1)} async-done(((bf16[8,1,256,512]{3,2,0,1:T(8,128)(2,1)}), bf16[2,1,256,512]{3,2,0,1:T(8,128)(2,1)}) %reduce-scatter.19.cloned.1.call-update) | async-done | bytes 524304 | tf_op jit(solution)/shard_map/reduce_scatter | solution.py:291
  926.6 14.6 %bitcast_convert_fusion = bf16[2048,2,2048]{2,0,1:T(8,128)(2,1)} fusion(bf16[2,256,2048,1]{2,1,0,3:T(8,128)(2,1)S(1)} %bitcast.464, bf16[2,256,1,2048]{3,1,0,2:T(8,128)(2,1)} %copy-done.37, bf16[2,256,1,2048]{3,1,0,2:T(8,128)(2,1)} %copy-done.36), kind=kOutput, calls=%fused_computation.58 | convolution fusion | flops 8606711808 | bytes 23068672 | tf_op jit(solution)/shard_map/spcd,spctf->dtf/dot_general | solution.py:219
  943.1 27.3 %reduce-scatter.29.cloned.1.call-done = bf16[2048,256]{1,0:T(8,128)(2,1)} async-done(((bf16[2048,2048]{1,0:T(8,128)(2,1)}), bf16[2048,256]{1,0:T(8,128)(2,1)}) %reduce-scatter.29.cloned.1.call-update) | async-done | bytes 1048592 | tf_op jit(solution)/shard_map/reduce_scatter | solution.py:234
  973.1 41.6 %reduce-scatter.25.cloned.1.call-done = bf16[512,256]{1,0:T(8,128)(2,1)} async-done(((bf16[512,2048]{1,0:T(8,128)(2,1)}), bf16[512,256]{1,0:T(8,128)(2,1)}) %reduce-scatter.25.cloned.1.call-update) | async-done | bytes 262160 | tf_op jit(solution)/shard_map/reduce_scatter | solution.py:325
  1016.5 77.7 %reduce-scatter.21.cloned.1.call-done = f32[1,2,64,2048]{3,2,1,0:T(8,128)} async-done(((f32[1,2,256,2048]{3,2,1,0:T(8,128)}), f32[1,2,64,2048]{3,2,1,0:T(8,128)}) %reduce-scatter.21.cloned.1.call-update) | async-done | bytes 1048592 | tf_op jit(solution)/shard_map/reduce_scatter | solution.py:74
  1095.9 13.6 all-reduce.3
  1122.1 51.9 %reduce-scatter.13.cloned.1.call-done = f32[1,2,64,2048]{3,2,1,0:T(8,128)} async-done(((f32[1,2,256,2048]{3,2,1,0:T(8,128)}), f32[1,2,64,2048]{3,2,1,0:T(8,128)}) %reduce-scatter.13.cloned.1.call-update) | async-done | bytes 1048592 | tf_op jit(solution)/shard_map/reduce_scatter | solution.py:66
  1177.1 62.2 %reduce-scatter.23.cloned.1.call-done = bf16[256,3,512]{2,0,1:T(8,128)(2,1)} async-done(((bf16[2048,3,512]{2,0,1:T(8,128)(2,1)}), bf16[256,3,512]{2,0,1:T(8,128)(2,1)}) %reduce-scatter.23.cloned.1.call-update) | async-done | bytes 786448 | tf_op jit(solution)/shard_map/reduce_scatter | solution.py:322
  1241.8 117.2 %reduce-scatter.27.cloned.1.call-done = bf16[256,2,2048]{2,0,1:T(8,128)(2,1)} async-done(((bf16[2048,2,2048]{2,0,1:T(8,128)(2,1)}), bf16[256,2,2048]{2,0,1:T(8,128)(2,1)}) %reduce-scatter.27.cloned.1.call-update) | async-done | bytes 2097168 | tf_op jit(solution)/shard_map/reduce_scatter | solution.py:231
  (451 shorter events, 447.0 us)
Async XLA Ops:
  7.2 80.8 %all-gather.11.cloned.1.call-start = ((), (), s32[]{:S(2)}) async-start(), calls=%async_computation.10 | async-start | bytes 7077888 | tf_op jit(solution)/shard_map/all_gather | solution.py:135
  7.9 133.5 %all-gather.13.cloned.1.call-start = ((), (), s32[]{:S(2)}) async-start(), calls=%async_computation.11 | async-start | bytes 2621440 | tf_op jit(solution)/shard_map/all_gather | solution.py:156
  21.6 14.2 %collective-permute-start = (bf16[1,1,2,64,2048]{4,3,2,1,0:T(8,128)(2,1)S(1)}, bf16[1,1,2,64,2048]{4,3,2,1,0:T(8,128)(2,1)S(1)}, u32[]{:S(2)}, u32[]{:S(2)}) collective-permute-start(bf16[1,1,2,64,2048]{4,3,2,1,0:T(8,128)(2,1)S(1)} %get-tuple-element.492), channel_id=1, source_target_pairs={{0,1},{1,0},{2,3},{3,2},{4,5},{5,4},{6,7},{7,6},{8,9},{9,8},{10,11... | collective-permute-start | bytes 1572872 | tf_op jit(solution)/shard_map/ppermute | solution.py:23
  36.4 48.1 %collective-permute-start.1 = (bf16[2,1,2,64,2048]{4,3,2,0,1:T(8,128)(2,1)S(1)}, bf16[2,1,2,64,2048]{4,3,2,0,1:T(8,128)(2,1)}, u32[]{:S(2)}, u32[]{:S(2)}) collective-permute-start(bf16[2,1,2,64,2048]{4,3,2,0,1:T(8,128)(2,1)S(1)} %get-tuple-element.490), channel_id=1, source_target_pairs={{0,2},{1,3},{2,0},{3,1},{4,6},{5,7},{6,4},{7,5},{8,10},{9,11},{10,... | collective-permute-start | bytes 3145736 | tf_op jit(solution)/shard_map/ppermute | solution.py:23
  118.4 47.7 %all-gather.15.cloned.1.call-start = ((), (), s32[]{:S(2)}) async-start(), calls=%async_computation.12 | async-start | bytes 2621440 | tf_op jit(solution)/shard_map/all_gather | solution.py:157
  122.1 141.0 %all-gather.17.cloned.1.call-start = ((), (), s32[]{:S(2)}) async-start(), calls=%async_computation.13 | async-start | bytes 2359296 | tf_op jit(solution)/shard_map/all_gather | solution.py:136
  122.7 222.7 %reduce-scatter.11.cloned.1.call-start = ((), (), s32[]{:S(2)}) async-start(), calls=%async_computation.14 | async-start | bytes 5242880 | tf_op jit(solution)/shard_map/reduce_scatter | solution.py:66
  268.2 169.8 %all-gather.19.cloned.1.call-start = ((), (), s32[]{:S(2)}) async-start(), calls=%async_computation.15 | async-start | bytes 18874368 | tf_op jit(solution)/shard_map/all_gather | solution.py:192
  272.0 213.2 %all-gather.23.cloned.1.call-start = ((), (), s32[]{:S(2)}) async-start(), calls=%async_computation.18 | async-start | bytes 2621440 | tf_op jit(solution)/shard_map/all_gather | solution.py:70
  272.8 269.0 %all-gather.21.cloned.1.call-start = ((), (), s32[]{:S(2)}) async-start(), calls=%async_computation.16 | async-start | bytes 9437184 | tf_op jit(solution)/shard_map/all_gather | solution.py:193
  273.6 372.3 %reduce-scatter.15.cloned.1.call-start = ((), (), s32[]{:S(2)}) async-start(), calls=%async_computation.19 | async-start | bytes 5242880 | tf_op jit(solution)/shard_map/reduce_scatter | solution.py:74
  346.8 300.7 %copy-start.1 = (f32[1,2,64,2048]{3,2,1,0:T(8,128)}, f32[1,2,64,2048]{3,2,1,0:T(8,128)S(1)}, u32[]{:S(2)}) copy-start(f32[1,2,64,2048]{3,2,1,0:T(8,128)S(1)} %get-tuple-element.460) | copy-start | bytes 3145732
  347.0 13.4 collective-permute-start.2
  360.7 48.0 %collective-permute-start.3 = (bf16[2,1,2,64,2048]{4,3,2,0,1:T(8,128)(2,1)S(1)}, bf16[2,1,2,64,2048]{4,3,2,0,1:T(8,128)(2,1)S(1)}, u32[]{:S(2)}, u32[]{:S(2)}) collective-permute-start(bf16[2,1,2,64,2048]{4,3,2,0,1:T(8,128)(2,1)S(1)} %get-tuple-element.484), channel_id=1, source_target_pairs={{0,2},{1,3},{2,0},{3,1},{4,6},{5,7},{6,4},{7,5},{8,10},{9,11},{10,... | collective-permute-start | bytes 3145736 | tf_op jit(solution)/shard_map/ppermute | solution.py:23
  568.9 126.1 %all-gather.25.cloned.1.call-start = ((), (), s32[]{:S(2)}) async-start(), calls=%async_computation.20 | async-start | bytes 2621440 | tf_op jit(solution)/shard_map/all_gather | solution.py:70
  648.7 212.8 %reduce-scatter.17.cloned.1.call-start = ((), (), s32[]{:S(2)}) async-start(), calls=%async_computation.21 | async-start | bytes 2621440 | tf_op jit(solution)/shard_map/reduce_scatter | solution.py:288
  831.3 64.3 %reduce-scatter.19.cloned.1.call-start = ((), (), s32[]{:S(2)}) async-start(), calls=%async_computation.22 | async-start | bytes 2621440 | tf_op jit(solution)/shard_map/reduce_scatter | solution.py:291
  831.9 138.5 %reduce-scatter.29.cloned.1.call-start = ((), (), s32[]{:S(2)}) async-start(), calls=%async_computation.27 | async-start | bytes 9437184 | tf_op jit(solution)/shard_map/reduce_scatter | solution.py:234
  841.3 173.4 %reduce-scatter.25.cloned.1.call-start = ((), (), s32[]{:S(2)}) async-start(), calls=%async_computation.25 | async-start | bytes 2359296 | tf_op jit(solution)/shard_map/reduce_scatter | solution.py:325
  845.6 248.6 %reduce-scatter.21.cloned.1.call-start = ((), (), s32[]{:S(2)}) async-start(), calls=%async_computation.23 | async-start | bytes 5242880 | tf_op jit(solution)/shard_map/reduce_scatter | solution.py:74
  904.2 269.7 %reduce-scatter.13.cloned.1.call-start = ((), (), s32[]{:S(2)}) async-start(), calls=%async_computation.17 | async-start | bytes 5242880 | tf_op jit(solution)/shard_map/reduce_scatter | solution.py:66
  916.9 322.4 %reduce-scatter.23.cloned.1.call-start = ((), (), s32[]{:S(2)}) async-start(), calls=%async_computation.24 | async-start | bytes 7077888 | tf_op jit(solution)/shard_map/reduce_scatter | solution.py:322
  925.1 434.0 %reduce-scatter.27.cloned.1.call-start = ((), (), s32[]{:S(2)}) async-start(), calls=%async_computation.26 | async-start | bytes 18874368 | tf_op jit(solution)/shard_map/reduce_scatter | solution.py:231
  943.1 230.9 %copy-start.2 = (f32[1,2,64,2048]{3,2,1,0:T(8,128)S(1)}, f32[1,2,64,2048]{3,2,1,0:T(8,128)}, u32[]{:S(2)}) copy-start(f32[1,2,64,2048]{3,2,1,0:T(8,128)} %copy-done.1) | copy-start | bytes 3145732
  (43 other events, 1412.1 us)
Sparse Core Ops, SparseCore 0:
  9.9 48.1 all-gather.10
  118.6 22.7 all-gather.12
  143.5 22.5 all-gather.14
  167.8 28.0 all-gather.16
  268.3 77.0 reduce-scatter.10
  347.7 90.2 all-gather.18
  439.5 45.6 all-gather.22
  487.1 54.6 all-gather.20
  569.0 76.7 reduce-scatter.14
  648.8 46.1 all-gather.24
  831.4 29.9 reduce-scatter.16
  864.4 31.1 reduce-scatter.18
  899.1 71.2 reduce-scatter.28
  973.5 41.1 reduce-scatter.24
  1017.4 76.7 reduce-scatter.20
  1096.4 77.5 reduce-scatter.12
  1177.2 62.0 reduce-scatter.22
  1242.8 116.2 reduce-scatter.26
